TPU v7x, 32 devices: a whole 2x2x4 slice. The times are simulated.
32 devices in a mesh: dom: 8 (over z, x), dp: 4 (over y, core).
Axes of the slice: x: 2, y: 2, z: 4, core: 2. Of those that a mesh axis runs over, the one named last changes fastest.
Arguments:
- node_latents: bfloat16 [32768, 128], P(('dom', 'dp')), may hold values from -6 to 6
- mesh_latents: bfloat16 [98304, 128], P(('dom', 'dp')), may hold values from -6 to 6
- world_latents: bfloat16 [16384, 128], P(('dom', 'dp')), may hold values from -6 to 6
- mesh_src: int32 [98304], P(('dom', 'dp')), may hold values from 0 to 1535, as said below
- mesh_dst: int32 [98304], P(('dom', 'dp')), may hold values from 0 to 1023
- world_src: int32 [16384], P(('dom', 'dp')), may hold values from 0 to 2047, as said below
- world_dst: int32 [16384], P(('dom', 'dp')), may hold values from 0 to 1023
- send_blocks: int32 [32, 8, 16], P(('dom', 'dp')), may hold values from 0 to 63
- world_count: int32 [32], P(('dom', 'dp')), may hold values from 256 to 512, as said below
- node_cot: bfloat16 [32768, 128], P(('dom', 'dp')), may hold values from -6 to 6
- mesh_cot: bfloat16 [98304, 128], P(('dom', 'dp')), may hold values from -6 to 6
- world_cot: bfloat16 [16384, 128], P(('dom', 'dp')), may hold values from -6 to 6
- first_weights: bfloat16 [3, 384, 128], replicated, may hold values from -0.3125 to 0.3125
- rest_weights: bfloat16 [3, 2, 128, 128], replicated, may hold values from -0.5 to 0.5
- biases: float32 [3, 4, 128], replicated, may hold values from -2 to 2
- gains: float32 [3, 128], replicated, may hold values from 0.1 to 1.9
Outputs:
- new_nodes: bfloat16 [32768, 128], P(('dom', 'dp'))
- new_mesh: bfloat16 [98304, 128], P(('dom', 'dp'))
- new_world: bfloat16 [16384, 128], P(('dom', 'dp'))
- grad_nodes: bfloat16 [32768, 128], P(('dom', 'dp'))
- grad_mesh: bfloat16 [98304, 128], P(('dom', 'dp'))
- grad_world: bfloat16 [16384, 128], P(('dom', 'dp'))
- grad_first: float32 [3, 384, 128], replicated
- grad_rest: float32 [3, 2, 128, 128], replicated
- grad_biases: float32 [3, 4, 128], replicated
- grad_gains: float32 [3, 128], replicated
Inputs may be any that keep to these rules, and one draw needn't show every extreme that they name: `mesh_src`: indexes the 256 rows before a partition's nodes (the last rows of the previous domain of its mesh), its 1024 nodes, then the 256 rows after (the first rows of the next domain); the first domain reads no rows before and the last none after. `world_src`: row j of slot t of the blocks sent by domain p of the same mesh is (p * 16 + t) * 16 + j; a partition reads some slots of each domain, all 16 for at least one. send_blocks[k, p, t] is the block of 16 node rows of partition k put in slot t for domain p of its mesh. Rows of partition k at or past world_count[k] are padding; some partition has all 512 rows live.
All inputs are finite; a program needn't handle non-finite values.
Results may differ from a plain program's by a relative error of at most 0.007.
Values may be sent and summed in bfloat16 or wider, within the bound.
No kernel may reach another device: no remote copies, remote signals or barrier semaphores. Data moves between devices by JAX's collectives and lax.ppermute only.
A program may use at most 128 MiB of HBM per device.

v0:
```python
import functools

import jax
import jax.numpy as jnp
from jax import lax
from jax.experimental import pallas as pl
from jax.experimental.pallas import tpu as pltpu
from jax.sharding import PartitionSpec as P

HALO = 256
BLK = 16
LANES = 128
PACK = 656

norm_eps = 1e-05
f32 = jnp.float32
bf16 = jnp.bfloat16


def dot(left, right):
    return jnp.dot(left, right, preferred_element_type=f32)


def dot_nt(left, right):
    return lax.dot_general(left, right, (((1,), (1,)), ((), ())), preferred_element_type=f32)


def dot_tn(left, right):
    return lax.dot_general(left, right, (((0,), (0,)), ((), ())), preferred_element_type=f32)


def sigmoid(values):
    return 0.5 * jnp.tanh(0.5 * values) + 0.5


def split(values):
    high = values.astype(bf16)
    low = (values - high.astype(f32)).astype(bf16)
    return jnp.concatenate([high, low], axis=1)


def joined(values):
    half = values.shape[1] // 2
    return values[:, :half] + values[:, half:]


def hot_rows(index, width):
    parts = []
    iota = lax.broadcasted_iota(jnp.int32, (LANES, width), 1)
    for row in range(index.shape[0]):
        column = jnp.broadcast_to(index[row : row + 1], (LANES, LANES)).T
        wide = jnp.concatenate([column] * (width // LANES), axis=1)
        parts.append(jnp.where(wide == iota, 1.0, 0.0).astype(bf16))
    return jnp.concatenate(parts, axis=0)


def hot_cols(index, first, width):
    iota = lax.broadcasted_iota(jnp.int32, (width, LANES), 0) + first
    parts = [
        jnp.where(jnp.broadcast_to(index[row : row + 1], (width, LANES)) == iota, 1.0, 0.0).astype(bf16)
        for row in range(index.shape[0])
    ]
    return jnp.concatenate(parts, axis=1)


def upper_layers(pre_one, rest_w, bias, gain):
    act_one = (pre_one * sigmoid(pre_one)).astype(bf16)
    pre_two = dot(act_one, rest_w[0]) + bias[1:2]
    act_two = (pre_two * sigmoid(pre_two)).astype(bf16)
    pre_three = dot(act_two, rest_w[1]) + bias[2:3]
    centred = pre_three - jnp.mean(pre_three, axis=-1, keepdims=True)
    inv_std = lax.rsqrt(jnp.mean(centred * centred, axis=-1, keepdims=True) + norm_eps)
    normed = centred * inv_std
    return normed * gain + bias[3:4], pre_two, normed, inv_std


def silu_parts(values):
    sigma = sigmoid(values)
    return (values * sigma).astype(bf16), sigma * (1.0 + values * (1.0 - sigma))


def backward_layers(cotangent, pre_one, pre_two, normed, inv_std, rest_w, gain):
    grad_gain = jnp.sum(cotangent * normed, axis=0, keepdims=True)
    grad_shift = jnp.sum(cotangent, axis=0, keepdims=True)
    scaled = cotangent * gain
    d_three = inv_std * (
        scaled
        - jnp.mean(scaled, axis=-1, keepdims=True)
        - normed * jnp.mean(scaled * normed, axis=-1, keepdims=True)
    )
    d_three_b = d_three.astype(bf16)
    act_two, slope_two = silu_parts(pre_two)
    grad_w3 = dot_tn(act_two, d_three_b)
    d_two = dot_nt(d_three_b, rest_w[1]) * slope_two
    d_two_b = d_two.astype(bf16)
    act_one, slope_one = silu_parts(pre_one)
    grad_w2 = dot_tn(act_one, d_two_b)
    d_one = dot_nt(d_two_b, rest_w[0]) * slope_one
    small = jnp.concatenate(
        [jnp.sum(d, axis=0, keepdims=True) for d in (d_one, d_two, d_three)] + [grad_shift, grad_gain],
        axis=0,
    )
    return d_one.astype(bf16), grad_w2, grad_w3, small


def send_kernel(blocks_ref, node_ref, out_ref):
    def one(step, _):
        source = pl.multiple_of(blocks_ref[step] * BLK, BLK)
        target = pl.multiple_of(step * BLK, BLK)
        out_ref[pl.ds(target, BLK), :] = node_ref[pl.ds(source, BLK), :]
        return 0

    lax.fori_loop(0, out_ref.shape[0] // BLK, one, 0, unroll=8)


def mesh_forward_kernel(
    lat_ref, before_ref, node_ref, after_ref, src_ref, dst_ref, first_ref, rest_ref, bias_ref, gain_ref,
    new_ref, one_ref, two_ref, norm_ref, inv_ref, sum_ref,
    table_src, table_dst, message_ref,
):
    tiles, groups = src_ref.shape[:2]
    tile = groups * LANES
    width = lat_ref.shape[1]
    nodes = node_ref.shape[0]
    halo = before_ref.shape[0]
    w_own = first_ref[0, :width]
    w_src = first_ref[0, width : 2 * width]
    w_dst = first_ref[0, 2 * width :]
    bias = bias_ref[0]
    gain = gain_ref[0:1]
    rest = (rest_ref[0, 0], rest_ref[0, 1])
    table_src[:halo] = split(dot(before_ref[...], w_src))
    table_src[halo : halo + nodes] = split(dot(node_ref[...], w_src))
    table_src[halo + nodes :] = split(dot(after_ref[...], w_src))
    table_dst[...] = split(dot(node_ref[...], w_dst))

    def one(step, _):
        rows = pl.ds(pl.multiple_of(step * tile, tile), tile)
        own = lat_ref[rows, :]
        gathered = dot(hot_rows(src_ref[step], nodes + 2 * halo), table_src[...])
        gathered = gathered + dot(hot_rows(dst_ref[step], nodes), table_dst[...])
        pre_one = dot(own, w_own) + joined(gathered) + bias[0:1]
        message, pre_two, normed, inv_std = upper_layers(pre_one, rest, bias, gain)
        new_ref[rows, :] = (own.astype(f32) + message).astype(bf16)
        one_ref[rows, :] = pre_one
        two_ref[rows, :] = pre_two
        norm_ref[rows, :] = normed
        inv_ref[rows, :] = jnp.broadcast_to(inv_std, normed.shape)
        message_ref[rows, :] = split(message)
        return 0

    lax.fori_loop(0, tiles, one, 0)
    block = 256

    def total(step, _):
        first = pl.multiple_of(step * block, block)
        hot = jnp.concatenate([hot_cols(dst_ref[t], first, block) for t in range(tiles)], axis=1)
        sum_ref[pl.ds(first, block), :] = joined(dot(hot, message_ref[...])).astype(bf16)
        return 0

    lax.fori_loop(0, nodes // block, total, 0)


def write_pack(ref, start, grad_first, grad_w2, grad_w3, small):
    wide, width = grad_first.shape
    ref[start : start + wide, :] = grad_first.astype(bf16)
    ref[start + wide : start + wide + width, :] = grad_w2.astype(bf16)
    ref[start + wide + width : start + wide + 2 * width, :] = grad_w3.astype(bf16)
    zeros = jnp.zeros((BLK - small.shape[0], width), f32)
    tail = start + wide + 2 * width
    ref[tail : tail + BLK, :] = jnp.concatenate([small, zeros], axis=0).astype(bf16)


def middle_kernel(
    count_ref, node_ref, lat_ref, incoming_ref, src_ref, dst_ref, sum_ref, node_cot_ref, world_cot_ref,
    first_ref, rest_ref, bias_ref, gain_ref,
    new_nodes_ref, new_world_ref, grad_world_ref, source_ref, local_ref, back_ref, pack_ref,
):
    nodes, width = node_ref.shape
    rows = lat_ref.shape[0]
    received = incoming_ref.shape[0]
    node = node_ref[...]
    keep = (lax.broadcasted_iota(jnp.int32, (rows, 1), 0) < count_ref[0]).astype(f32)

    src = src_ref[...]
    dst = dst_ref[...]
    lat = lat_ref[...]
    hot_dst = hot_rows(dst, nodes)
    x_src = dot(hot_rows(src, received), incoming_ref[...]).astype(bf16)
    x_dst = dot(hot_dst, node).astype(bf16)
    w_inputs = jnp.concatenate([lat, x_src, x_dst], axis=1)
    w_rest = (rest_ref[1, 0], rest_ref[1, 1])
    w_one = dot(w_inputs, first_ref[1]) + bias_ref[1][0:1]
    message, w_two, w_norm, w_inv = upper_layers(w_one, w_rest, bias_ref[1], gain_ref[1:2])
    message = message * keep
    new_world_ref[...] = (lat.astype(f32) + message).astype(bf16)
    world_sum = joined(dot(hot_cols(dst, 0, nodes), split(message))).astype(bf16)

    n_inputs = jnp.concatenate([node, sum_ref[...], world_sum], axis=1)
    n_rest = (rest_ref[2, 0], rest_ref[2, 1])
    n_one = dot(n_inputs, first_ref[2]) + bias_ref[2][0:1]
    update, n_two, n_norm, n_inv = upper_layers(n_one, n_rest, bias_ref[2], gain_ref[2:3])
    new_nodes_ref[...] = (node.astype(f32) + update).astype(bf16)
    node_cot = node_cot_ref[...].astype(f32)
    d_one, grad_w2, grad_w3, small = backward_layers(
        node_cot, n_one, n_two, n_norm, n_inv, n_rest, gain_ref[2:3]
    )
    write_pack(pack_ref, PACK, dot_tn(n_inputs, d_one), grad_w2, grad_w3, small)
    node_back = dot_nt(d_one, first_ref[2])
    local_ref[...] = node_cot + node_back[:, :width]
    back_ref[...] = split(node_back[:, width : 2 * width])
    world_back = split(node_back[:, 2 * width :])

    world_cot = world_cot_ref[...].astype(f32)
    upstream = keep * (world_cot + joined(dot(hot_dst, world_back)))
    d_one, grad_w2, grad_w3, small = backward_layers(
        upstream, w_one, w_two, w_norm, w_inv, w_rest, gain_ref[1:2]
    )
    write_pack(pack_ref, 0, dot_tn(w_inputs, d_one), grad_w2, grad_w3, small)
    in_grad = dot_nt(d_one, first_ref[1])
    grad_world_ref[...] = (world_cot + in_grad[:, :width]).astype(bf16)
    to_source = split(in_grad[:, width : 2 * width])
    to_target = split(in_grad[:, 2 * width :])
    local_ref[...] += joined(dot(hot_cols(dst, 0, nodes), to_target))
    block = 512

    def back(step, _):
        first = pl.multiple_of(step * block, block)
        source_ref[pl.ds(first, block), :] = joined(dot(hot_cols(src_ref[...], first, block), to_source)).astype(bf16)
        return 0

    lax.fori_loop(0, received // block, back, 0)


def mesh_backward_kernel(
    lat_ref, before_ref, node_ref, after_ref, src_ref, dst_ref, cot_ref, back_ref,
    one_ref, two_ref, norm_ref, inv_ref, local_ref, first_ref, rest_ref, gain_ref,
    grad_ref, left_ref, right_ref, out_ref, pack_ref,
    d_ref, w1_acc, w2_acc, w3_acc, small_acc, sum_src,
):
    tiles, groups = src_ref.shape[:2]
    tile = groups * LANES
    width = lat_ref.shape[1]
    nodes = node_ref.shape[0]
    halo = before_ref.shape[0]
    w_own = first_ref[0, :width]
    w_src = first_ref[0, width : 2 * width]
    w_dst = first_ref[0, 2 * width :]
    gain = gain_ref[0:1]
    rest = (rest_ref[0, 0], rest_ref[0, 1])
    for ref in (w1_acc, w2_acc, w3_acc, small_acc):
        ref[...] = jnp.zeros(ref.shape, f32)

    def one(step, _):
        rows = pl.ds(pl.multiple_of(step * tile, tile), tile)
        cot = cot_ref[rows, :].astype(f32)
        upstream = cot + joined(dot(hot_rows(dst_ref[step], nodes), back_ref[...]))
        d_one, grad_w2, grad_w3, small = backward_layers(
            upstream, one_ref[rows, :], two_ref[rows, :], norm_ref[rows, :], inv_ref[rows, :], rest, gain
        )
        d_ref[rows, :] = d_one
        w1_acc[...] += dot_tn(lat_ref[rows, :], d_one)
        w2_acc[...] += grad_w2
        w3_acc[...] += grad_w3
        small_acc[0 : small.shape[0], :] += small
        grad_ref[rows, :] = (cot + dot_nt(d_one, w_own)).astype(bf16)
        return 0

    lax.fori_loop(0, tiles, one, 0)
    block = 256

    def scattered(index_ref, first):
        hot = jnp.concatenate([hot_cols(index_ref[t], first, block) for t in range(tiles)], axis=1)
        return split(dot(hot, d_ref[...]))

    def source(step, total):
        first = pl.multiple_of(step * block, block)
        sum_src[pl.ds(first, block), :] = scattered(src_ref, first)
        return total

    lax.fori_loop(0, (nodes + 2 * halo) // block, source, 0)

    def target(step, total):
        first = pl.multiple_of(step * block, block)
        here = pl.ds(first, block)
        sums = scattered(dst_ref, first)
        inner = sum_src[pl.ds(pl.multiple_of(first + halo, block), block), :]
        grad = dot_nt(sums[:, :width], w_dst) + dot_nt(sums[:, width:], w_dst)
        grad = grad + dot_nt(inner[:, :width], w_src) + dot_nt(inner[:, width:], w_src)
        out_ref[here, :] = local_ref[here, :] + grad
        return total + dot_tn(node_ref[here, :], sums)

    grad_dst = joined(lax.fori_loop(0, nodes // block, target, jnp.zeros((width, 2 * width), f32)))
    first_rows = sum_src[:halo]
    last_rows = sum_src[halo + nodes :]
    left_ref[...] = (dot_nt(first_rows[:, :width], w_src) + dot_nt(first_rows[:, width:], w_src)).astype(bf16)
    right_ref[...] = (dot_nt(last_rows[:, :width], w_src) + dot_nt(last_rows[:, width:], w_src)).astype(bf16)
    grad_src = dot_tn(before_ref[...], first_rows) + dot_tn(node_ref[...], sum_src[halo : halo + nodes])
    grad_src = joined(grad_src + dot_tn(after_ref[...], last_rows))
    grad_first = jnp.concatenate([w1_acc[...], grad_src, grad_dst], axis=0)
    write_pack(pack_ref, 0, grad_first, w2_acc[...], w3_acc[...], small_acc[0:5, :])


def final_kernel(blocks_ref, local_ref, left_ref, right_ref, returned_ref, out_ref, total_ref):
    nodes = local_ref.shape[0]
    halo = left_ref.shape[0]
    total_ref[...] = local_ref[...]
    total_ref[:halo] += left_ref[...].astype(f32)
    total_ref[nodes - halo :] += right_ref[...].astype(f32)

    def one(step, _):
        target = pl.ds(pl.multiple_of(blocks_ref[step] * BLK, BLK), BLK)
        source = pl.ds(pl.multiple_of(step * BLK, BLK), BLK)
        total_ref[target, :] += returned_ref[source, :].astype(f32)
        return 0

    lax.fori_loop(0, returned_ref.shape[0] // BLK, one, 0, unroll=8)
    out_ref[...] = total_ref[...].astype(bf16)


def call(kernel, outs, operands, scalars=0, scratch=(), name=None):
    specs = [pl.BlockSpec(memory_space=pltpu.SMEM)] * scalars
    specs += [pl.BlockSpec(memory_space=pltpu.VMEM)] * (len(operands) - scalars)
    return pl.pallas_call(
        kernel,
        out_shape=[jax.ShapeDtypeStruct(shape, kind) for shape, kind in outs],
        in_specs=specs,
        out_specs=[pl.BlockSpec(memory_space=pltpu.VMEM)] * len(outs),
        scratch_shapes=list(scratch),
        name=name,
    )(*operands)


def per_device(
    node_latents,
    mesh_latents,
    world_latents,
    mesh_src,
    mesh_dst,
    world_src,
    world_dst,
    send_blocks,
    world_count,
    node_cot,
    mesh_cot,
    world_cot,
    first_weights,
    rest_weights,
    biases,
    gains,
):
    nodes, width = node_latents.shape
    edges = mesh_latents.shape[0]
    world_rows = world_latents.shape[0]
    domains = lax.axis_size("dom")
    devices = domains * lax.axis_size("dp")
    both = ("dom", "dp")
    up = [(i, i + 1) for i in range(domains - 1)]
    down = [(j, i) for i, j in up]
    blocks = send_blocks.reshape(-1)
    received = blocks.shape[0] * BLK

    (outgoing,) = call(send_kernel, [((received, width), bf16)], (blocks, node_latents), scalars=1, name="send")
    incoming = lax.all_to_all(outgoing, "dom", split_axis=0, concat_axis=0, tiled=True)
    before = lax.ppermute(node_latents[nodes - HALO :], "dom", up)
    after = lax.ppermute(node_latents[:HALO], "dom", down)

    tile = 4 * LANES
    src = mesh_src.reshape(edges // tile, tile // LANES, LANES)
    dst = mesh_dst.reshape(edges // tile, tile // LANES, LANES)
    full = ((edges, width), f32)
    new_mesh, pre_one, pre_two, normed, inv_std, mesh_sum = call(
        mesh_forward_kernel,
        [((edges, width), bf16), full, full, full, full, ((nodes, width), bf16)],
        (mesh_latents, before, node_latents, after, src, dst, first_weights, rest_weights, biases, gains),
        scratch=[
            pltpu.VMEM((nodes + 2 * HALO, 2 * width), bf16),
            pltpu.VMEM((nodes, 2 * width), bf16),
            pltpu.VMEM((edges, 2 * width), bf16),
        ],
        name="mesh_forward",
    )
    new_nodes, new_world, grad_world, to_source, local, mesh_back, early = call(
        middle_kernel,
        [
            ((nodes, width), bf16),
            ((world_rows, width), bf16),
            ((world_rows, width), bf16),
            ((received, width), bf16),
            ((nodes, width), f32),
            ((nodes, 2 * width), bf16),
            ((2 * PACK, width), bf16),
        ],
        (
            world_count,
            node_latents,
            world_latents,
            incoming,
            world_src.reshape(-1, LANES),
            world_dst.reshape(-1, LANES),
            mesh_sum,
            node_cot,
            world_cot,
            first_weights,
            rest_weights,
            biases,
            gains,
        ),
        scalars=1,
        name="middle",
    )
    returned = lax.all_to_all(to_source, "dom", split_axis=0, concat_axis=0, tiled=True)
    grad_mesh, to_left, to_right, local, late = call(
        mesh_backward_kernel,
        [
            ((edges, width), bf16),
            ((HALO, width), bf16),
            ((HALO, width), bf16),
            ((nodes, width), f32),
            ((PACK, width), bf16),
        ],
        (
            mesh_latents,
            before,
            node_latents,
            after,
            src,
            dst,
            mesh_cot,
            mesh_back,
            pre_one,
            pre_two,
            normed,
            inv_std,
            local,
            first_weights,
            rest_weights,
            gains,
        ),
        scratch=[
            pltpu.VMEM((edges, width), bf16),
            pltpu.VMEM((width, width), f32),
            pltpu.VMEM((width, width), f32),
            pltpu.VMEM((width, width), f32),
            pltpu.VMEM((8, width), f32),
            pltpu.VMEM((nodes + 2 * HALO, 2 * width), bf16),
        ],
        name="mesh_backward",
    )
    from_right = lax.ppermute(to_left, "dom", down)
    from_left = lax.ppermute(to_right, "dom", up)

    share = -(-3 * PACK // devices)
    share = -(-share // 16) * 16
    padding = jnp.zeros((share * devices - 3 * PACK, width), bf16)
    packed = jnp.concatenate([late, early, padding], axis=0)
    parts = lax.all_to_all(packed, both, split_axis=0, concat_axis=0, tiled=True)
    mine = jnp.sum(parts.reshape(devices, share, width).astype(f32), axis=0).astype(bf16)
    spread = jnp.broadcast_to(mine[None], (devices, share, width)).reshape(devices * share, width)
    spread = lax.all_to_all(spread, both, split_axis=0, concat_axis=0, tiled=True)
    sums = spread[: 3 * PACK].reshape(3, PACK, width).astype(f32) / devices
    (grad_nodes,) = call(
        final_kernel,
        [((nodes, width), bf16)],
        (blocks, local, from_left, from_right, returned),
        scalars=1,
        scratch=[pltpu.VMEM((nodes, width), f32)],
        name="final",
    )
    wide = 3 * width
    return (
        new_nodes,
        new_mesh,
        new_world,
        grad_nodes,
        grad_mesh,
        grad_world,
        sums[:, :wide],
        sums[:, wide : wide + 2 * width].reshape(3, 2, width, width),
        sums[:, wide + 2 * width : wide + 2 * width + 4],
        sums[:, wide + 2 * width + 4],
    )


def solution(mesh):
    rows = P(("dom", "dp"), None)
    flat = P(("dom", "dp"))
    return jax.shard_map(
        per_device,
        mesh=mesh,
        in_specs=(
            rows,
            rows,
            rows,
            flat,
            flat,
            flat,
            flat,
            P(("dom", "dp"), None, None),
            flat,
            rows,
            rows,
            rows,
            P(),
            P(),
            P(),
            P(),
        ),
        out_specs=(rows, rows, rows, rows, rows, rows, P(), P(), P(), P()),
        check_vma=False,
    )
```

profile of v0, /device:TPU:17, one launch (start us, length us, event | category | flops | bytes accessed | tf_op | source)
XLA Modules:
  0.0 137.0 jit_solution(5387700284414322310)
XLA Ops:
  0.7 1.3 reshape.55.blocks_ref
  2.0 2.2 %send.1 = bf16[2048,128]{1,0:T(8,128)(2,1)} custom-call(s32[128]{0:T(128)} %reshape.55.blocks_ref, bf16[1024,128]{1,0:T(8,128)(2,1)} %node_ref.7), custom_call_target="tpu_custom_call" | custom-call | tf_op jit(solution)/shard_map/send/pallas_call | solution.py:324
  4.1 5.6 %all-to-all-start = ((bf16[8,256,128]{2,1,0:T(8,128)(2,1)}), bf16[8,256,128]{2,1,0:T(8,128)(2,1)S(1)}, u32[]{:S(2)}, u32[]{:S(2)}) async-start(bf16[8,256,128]{2,1,0:T(8,128)(2,1)} %bitcast.21), calls=%async_computation | async-start | bytes 1048576 | tf_op jit(solution)/shard_map/all_to_all | solution.py:364
  9.7 3.1 %collective-permute-start = (bf16[256,128]{1,0:T(8,128)(2,1)S(1)}, bf16[256,128]{1,0:T(8,128)(2,1)S(1)}, u32[]{:S(2)}, u32[]{:S(2)}) collective-permute-start(bf16[256,128]{1,0:T(8,128)(2,1)S(1)} %get-tuple-element.57), channel_id=1, source_target_pairs={{0,4},{4,8},{8,12},{12,16},{16,20},{20,24},{24,28},{1,5},{5,9},{9,... | collective-permute-start | bytes 196616 | tf_op jit(solution)/shard_map/ppermute | solution.py:365
  12.8 3.1 %collective-permute-start.1 = (bf16[256,128]{1,0:T(8,128)(2,1)S(1)}, bf16[256,128]{1,0:T(8,128)(2,1)S(1)}, u32[]{:S(2)}, u32[]{:S(2)}) collective-permute-start(bf16[256,128]{1,0:T(8,128)(2,1)S(1)} %get-tuple-element.56), channel_id=1, source_target_pairs={{4,0},{8,4},{12,8},{16,12},{20,16},{24,20},{28,24},{5,1},{9,5},{13... | collective-permute-start | bytes 196616 | tf_op jit(solution)/shard_map/ppermute | solution.py:366
  16.7 8.2 %collective-permute-done.before_ref = bf16[256,128]{1,0:T(8,128)(2,1)S(1)} collective-permute-done((bf16[256,128]{1,0:T(8,128)(2,1)S(1)}, bf16[256,128]{1,0:T(8,128)(2,1)S(1)}, u32[]{:S(2)}, u32[]{:S(2)}) %collective-permute-start) | collective-permute-done | bytes 65568 | tf_op jit(solution)/shard_map/ppermute | solution.py:365
  24.9 0.6 copy-done.4
  25.6 15.1 %mesh_forward.1 = (bf16[3072,128]{1,0:T(8,128)(2,1)}, f32[3072,128]{1,0:T(8,128)}, f32[3072,128]{1,0:T(8,128)}, f32[3072,128]{1,0:T(8,128)}, f32[3072,128]{1,0:T(8,128)}, /*index=5*/bf16[1024,128]{1,0:T(8,128)(2,1)}) custom-call(bf16[3072,128]{1,0:T(8,128)(2,1)} %lat_ref.5, bf16[256,128]{1,0:T(8,128)(2,1)} %copy-done.4, bf16[1024,128]{1,0:T(8,128)(2,1)} %node_ref.7, ...), custom_call_target="tpu_custom_call" | custom-call | tf_op jit(solution)/shard_map/mesh_forward/pallas_call | solution.py:324
  40.7 0.8 copy-done.1
  41.4 10.4 %middle.1 = (bf16[1024,128]{1,0:T(8,128)(2,1)}, bf16[512,128]{1,0:T(8,128)(2,1)}, bf16[512,128]{1,0:T(8,128)(2,1)}, bf16[2048,128]{1,0:T(8,128)(2,1)}, f32[1024,...) custom-call(s32[1]{0:T(128)S(6)} %copy.31.count_ref, bf16[1024,128]{1,0:T(8,128)(2,1)} %node_ref.7, ...), custom_call_target="tpu_custom_call" | custom-call | tf_op jit(solution)/shard_map/middle/pallas_call | solution.py:324
  51.9 20.5 %mesh_backward.1 = (bf16[3072,128]{1,0:T(8,128)(2,1)}, bf16[256,128]{1,0:T(8,128)(2,1)}, bf16[256,128]{1,0:T(8,128)(2,1)}, f32[1024,128]{1,0:T(8,128)}, bf16[656,128]{1,0:T(8,128)(2,1)}) custom-call(bf16[3072,128]{1,0:T(8,128)(2,1)} %lat_ref.5, bf16[256,128]{1,0:T(8,128)(2,1)} %copy-done.4, bf16[1024,128]{1,0:T(8,128)(2,1)} %node_ref.7, ...), custom_call_target="tpu_custom_call" | custom-call | tf_op jit(solution)/shard_map/mesh_backward/pallas_call | solution.py:324
  72.4 1.3 maximum_maximum_fusion
  73.7 18.1 %all_to_all.40 = bf16[32,64,128]{2,1,0:T(8,128)(2,1)S(1)} all-to-all(bf16[32,64,128]{2,1,0:T(8,128)(2,1)S(1)} %bitcast.22), channel_id=1, replica_groups=mesh['dom'=8,'dp'=4] {'dom','dp'}, dimensions={0} | all-to-all | bytes 1048576 | tf_op jit(solution)/shard_map/all_to_all | solution.py:457
  91.8 4.7 %all-to-all-start.1 = ((bf16[8,256,128]{2,1,0:T(8,128)(2,1)}), bf16[8,256,128]{2,1,0:T(8,128)(2,1)S(1)}, u32[]{:S(2)}, u32[]{:S(2)}) async-start(bf16[8,256,128]{2,1,0:T(8,128)(2,1)} %bitcast.6), calls=%async_computation.1 | async-start | bytes 1048576 | tf_op jit(solution)/shard_map/all_to_all | solution.py:412
  96.5 12.3 %all-to-all-done.1 = bf16[8,256,128]{2,1,0:T(8,128)(2,1)S(1)} async-done(((bf16[8,256,128]{2,1,0:T(8,128)(2,1)}), bf16[8,256,128]{2,1,0:T(8,128)(2,1)S(1)}, u32[]{:S(2)}, u32[]{:S(2)}) %all-to-all-start.1) | async-done | bytes 524320 | tf_op jit(solution)/shard_map/all_to_all | solution.py:412
  108.8 1.0 broadcast_in_dim.10
  109.8 6.3 %all-to-all-start.3 = ((bf16[32,64,128]{2,1,0:T(8,128)(2,1)}), bf16[32,64,128]{2,1,0:T(8,128)(2,1)S(1)}, u32[]{:S(2)}, u32[]{:S(2)}) async-start(bf16[32,64,128]{2,1,0:T(8,128)(2,1)} %broadcast_in_dim.10), calls=%async_computation.3 | async-start | bytes 1048576 | tf_op jit(solution)/shard_map/all_to_all | solution.py:460
  116.0 3.1 %collective-permute-start.2 = (bf16[256,128]{1,0:T(8,128)(2,1)S(1)}, bf16[256,128]{1,0:T(8,128)(2,1)S(1)}, u32[]{:S(2)}, u32[]{:S(2)}) collective-permute-start(bf16[256,128]{1,0:T(8,128)(2,1)S(1)} %copy-done.9), channel_id=1, source_target_pairs={{0,4},{4,8},{8,12},{12,16},{16,20},{20,24},{24,28},{1,5},{5,9},{9,... | collective-permute-start | bytes 196616 | tf_op jit(solution)/shard_map/ppermute | solution.py:451
  119.2 3.1 %collective-permute-start.3 = (bf16[256,128]{1,0:T(8,128)(2,1)S(1)}, bf16[256,128]{1,0:T(8,128)(2,1)S(1)}, u32[]{:S(2)}, u32[]{:S(2)}) collective-permute-start(bf16[256,128]{1,0:T(8,128)(2,1)S(1)} %copy-done.8), channel_id=1, source_target_pairs={{4,0},{8,4},{12,8},{16,12},{20,16},{24,20},{28,24},{5,1},{9,5},{13... | collective-permute-start | bytes 196616 | tf_op jit(solution)/shard_map/ppermute | solution.py:450
  122.2 8.8 %collective-permute-done.2.left_ref = bf16[256,128]{1,0:T(8,128)(2,1)S(1)} collective-permute-done((bf16[256,128]{1,0:T(8,128)(2,1)S(1)}, bf16[256,128]{1,0:T(8,128)(2,1)S(1)}, u32[]{:S(2)}, u32[]{:S(2)}) %collective-permute-start.2) | collective-permute-done | bytes 65568 | tf_op jit(solution)/shard_map/ppermute | solution.py:451
  131.0 0.6 copy-done.6
  131.6 2.5 %final.1 = bf16[1024,128]{1,0:T(8,128)(2,1)} custom-call(s32[128]{0:T(128)} %reshape.55.blocks_ref, f32[1024,128]{1,0:T(8,128)} %get-tuple-element.38.local_ref, bf16[256,128]{1,0:T(8,128)(2,1)} %copy-done.6, bf16[256,128]{1,0:T(8,128)(2,1)} %copy-done.7, bf16[2048,128]{1,0:T(8,128)(2,1)} %bitcast.20), custom_call_target="tpu_custom_call" | custom-call | tf_op jit(solution)/shard_map/final/pallas_call | solution.py:324
  134.2 0.9 slice.29
  135.1 0.8 slice.30
  (29 shorter events, 1.5 us)
Async XLA Ops:
  0.6 9.1 %copy-start = (bf16[1024,128]{1,0:T(8,128)(2,1)S(1)}, bf16[1024,128]{1,0:T(8,128)(2,1)}, u32[]{:S(2)}) copy-start(bf16[1024,128]{1,0:T(8,128)(2,1)} %node_ref.7) | copy-start | bytes 786436
  4.1 36.5 %all-to-all-start = ((bf16[8,256,128]{2,1,0:T(8,128)(2,1)}), bf16[8,256,128]{2,1,0:T(8,128)(2,1)S(1)}, u32[]{:S(2)}, u32[]{:S(2)}) async-start(bf16[8,256,128]{2,1,0:T(8,128)(2,1)} %bitcast.21), calls=%async_computation | async-start | bytes 1048576 | tf_op jit(solution)/shard_map/all_to_all | solution.py:364
  9.7 15.2 %collective-permute-start = (bf16[256,128]{1,0:T(8,128)(2,1)S(1)}, bf16[256,128]{1,0:T(8,128)(2,1)S(1)}, u32[]{:S(2)}, u32[]{:S(2)}) collective-permute-start(bf16[256,128]{1,0:T(8,128)(2,1)S(1)} %get-tuple-element.57), channel_id=1, source_target_pairs={{0,4},{4,8},{8,12},{12,16},{16,20},{20,24},{24,28},{1,5},{5,9},{9,... | collective-permute-start | bytes 196616 | tf_op jit(solution)/shard_map/ppermute | solution.py:365
  12.8 12.1 %collective-permute-start.1 = (bf16[256,128]{1,0:T(8,128)(2,1)S(1)}, bf16[256,128]{1,0:T(8,128)(2,1)S(1)}, u32[]{:S(2)}, u32[]{:S(2)}) collective-permute-start(bf16[256,128]{1,0:T(8,128)(2,1)S(1)} %get-tuple-element.56), channel_id=1, source_target_pairs={{4,0},{8,4},{12,8},{16,12},{20,16},{24,20},{28,24},{5,1},{9,5},{13... | collective-permute-start | bytes 196616 | tf_op jit(solution)/shard_map/ppermute | solution.py:366
  24.9 0.6 copy-start.4
  24.9 0.7 copy-start.5
  40.7 0.8 copy-start.1
  51.9 20.5 %copy-start.3 = (bf16[1312,128]{1,0:T(8,128)(2,1)S(1)}, bf16[1312,128]{1,0:T(8,128)(2,1)}, u32[]{:S(2)}) copy-start(bf16[1312,128]{1,0:T(8,128)(2,1)} %get-tuple-element.45) | copy-start | bytes 1007620
  91.7 24.3 %copy-start.9 = (bf16[256,128]{1,0:T(8,128)(2,1)S(1)}, bf16[256,128]{1,0:T(8,128)(2,1)}, u32[]{:S(2)}) copy-start(bf16[256,128]{1,0:T(8,128)(2,1)} %get-tuple-element.39) | copy-start | bytes 196612
  91.8 27.4 %copy-start.8 = (bf16[256,128]{1,0:T(8,128)(2,1)S(1)}, bf16[256,128]{1,0:T(8,128)(2,1)}, u32[]{:S(2)}) copy-start(bf16[256,128]{1,0:T(8,128)(2,1)} %get-tuple-element.40) | copy-start | bytes 196612
  91.8 17.0 %all-to-all-start.1 = ((bf16[8,256,128]{2,1,0:T(8,128)(2,1)}), bf16[8,256,128]{2,1,0:T(8,128)(2,1)S(1)}, u32[]{:S(2)}, u32[]{:S(2)}) async-start(bf16[8,256,128]{2,1,0:T(8,128)(2,1)} %bitcast.6), calls=%async_computation.1 | async-start | bytes 1048576 | tf_op jit(solution)/shard_map/all_to_all | solution.py:412
  108.8 22.2 %copy-start.2 = (bf16[8,256,128]{2,1,0:T(8,128)(2,1)}, bf16[8,256,128]{2,1,0:T(8,128)(2,1)S(1)}, u32[]{:S(2)}) copy-start(bf16[8,256,128]{2,1,0:T(8,128)(2,1)S(1)} %all-to-all-done.1) | copy-start | bytes 1572868
  109.8 24.4 %all-to-all-start.3 = ((bf16[32,64,128]{2,1,0:T(8,128)(2,1)}), bf16[32,64,128]{2,1,0:T(8,128)(2,1)S(1)}, u32[]{:S(2)}, u32[]{:S(2)}) async-start(bf16[32,64,128]{2,1,0:T(8,128)(2,1)} %broadcast_in_dim.10), calls=%async_computation.3 | async-start | bytes 1048576 | tf_op jit(solution)/shard_map/all_to_all | solution.py:460
  116.0 15.0 %collective-permute-start.2 = (bf16[256,128]{1,0:T(8,128)(2,1)S(1)}, bf16[256,128]{1,0:T(8,128)(2,1)S(1)}, u32[]{:S(2)}, u32[]{:S(2)}) collective-permute-start(bf16[256,128]{1,0:T(8,128)(2,1)S(1)} %copy-done.9), channel_id=1, source_target_pairs={{0,4},{4,8},{8,12},{12,16},{16,20},{20,24},{24,28},{1,5},{5,9},{9,... | collective-permute-start | bytes 196616 | tf_op jit(solution)/shard_map/ppermute | solution.py:451
  119.2 11.9 %collective-permute-start.3 = (bf16[256,128]{1,0:T(8,128)(2,1)S(1)}, bf16[256,128]{1,0:T(8,128)(2,1)S(1)}, u32[]{:S(2)}, u32[]{:S(2)}) collective-permute-start(bf16[256,128]{1,0:T(8,128)(2,1)S(1)} %copy-done.8), channel_id=1, source_target_pairs={{4,0},{8,4},{12,8},{16,12},{20,16},{24,20},{28,24},{5,1},{9,5},{13... | collective-permute-start | bytes 196616 | tf_op jit(solution)/shard_map/ppermute | solution.py:450
  131.0 0.6 copy-start.6
  131.0 0.6 copy-start.7
where the time goes:
time: 138 us; the launch traced here: 137 us
  Pallas kernels  50.7 us (37%)
  waiting for transfers between devices  29.2 us (21%)
  starting transfers between devices  28.9 us (21%)
  blocking collectives  18.1 us (13%)
  local copies, waits for them, and re-layouts  7.3 us (5%)
  other arithmetic  1.41 us (1%)
  between operations  1.41 us (1%)
    pallas_call x5, Pallas kernels, call(): pl.pallas_call(kernel, out_shape=[jax.ShapeDtypeStruct(shape, kind) for s...  50.7 us
    all_to_all x1, blocking collectives, per_device(): lax.all_to_all(packed, both, split_axis=0, concat_axis=0, tiled=True)  18.1 us
    all_to_all x1, waiting for transfers between devices, per_device(): lax.all_to_all(to_source, 'dom', split_axis=0, concat_axis=0, tiled=True)  12.3 us
    ppermute x1, waiting for transfers between devices, per_device(): from_left = lax.ppermute(to_right, 'dom', up)  8.76 us
    ppermute x1, waiting for transfers between devices, per_device(): before = lax.ppermute(node_latents[nodes - HALO:], 'dom', up)  8.22 us
    all_to_all x1, starting transfers between devices, per_device(): lax.all_to_all(spread, both, split_axis=0, concat_axis=0, tiled=True)  6.25 us
    all_to_all x1, starting transfers between devices, per_device(): lax.all_to_all(outgoing, 'dom', split_axis=0, concat_axis=0, tiled=True)  5.58 us
    all_to_all x1, starting transfers between devices, per_device(): lax.all_to_all(to_source, 'dom', split_axis=0, concat_axis=0, tiled=True)  4.69 us
  transfers between devices with their start and end apart: 7, of which 3 were waited for; matrix products, arithmetic and copies ran while one was open for 0% of the time, Pallas kernels for 13%

commit v1 on v0

--- a/solution.py
+++ b/solution.py
@@ -7,10 +7,12 @@
 from jax.experimental.pallas import tpu as pltpu
 from jax.sharding import PartitionSpec as P
 
+
 HALO = 256
 BLK = 16
 LANES = 128
 PACK = 656
+COST = 250
 
 norm_eps = 1e-05
 f32 = jnp.float32
@@ -104,19 +106,22 @@
 
 
 def send_kernel(blocks_ref, node_ref, out_ref):
-    def one(step, _):
-        source = pl.multiple_of(blocks_ref[step] * BLK, BLK)
-        target = pl.multiple_of(step * BLK, BLK)
-        out_ref[pl.ds(target, BLK), :] = node_ref[pl.ds(source, BLK), :]
-        return 0
-
-    lax.fori_loop(0, out_ref.shape[0] // BLK, one, 0, unroll=8)
+    _, domains, slots = blocks_ref.shape
+
+    def one(domain, _):
+        for slot in range(slots):
+            source = pl.multiple_of(blocks_ref[0, domain, slot] * BLK, BLK)
+            target = pl.multiple_of((domain * slots + slot) * BLK, BLK)
+            out_ref[pl.ds(target, BLK), :] = node_ref[pl.ds(source, BLK), :]
+        return 0
+
+    lax.fori_loop(0, domains, one, 0)
 
 
 def mesh_forward_kernel(
     lat_ref, before_ref, node_ref, after_ref, src_ref, dst_ref, first_ref, rest_ref, bias_ref, gain_ref,
-    new_ref, one_ref, two_ref, norm_ref, inv_ref, sum_ref,
-    table_src, table_dst, message_ref,
+    new_ref, sum_ref, saved_refs,
+    table_src, table_dst, message_ref, saves, sems,
 ):
     tiles, groups = src_ref.shape[:2]
     tile = groups * LANES
@@ -142,10 +147,9 @@
         pre_one = dot(own, w_own) + joined(gathered) + bias[0:1]
         message, pre_two, normed, inv_std = upper_layers(pre_one, rest, bias, gain)
         new_ref[rows, :] = (own.astype(f32) + message).astype(bf16)
-        one_ref[rows, :] = pre_one
-        two_ref[rows, :] = pre_two
-        norm_ref[rows, :] = normed
-        inv_ref[rows, :] = jnp.broadcast_to(inv_std, normed.shape)
+        for which, value in enumerate((pre_one, pre_two, normed, jnp.broadcast_to(inv_std, normed.shape))):
+            saves[which, rows, :] = value
+            pltpu.make_async_copy(saves.at[which, rows], saved_refs.at[which, rows], sems.at[step, which]).start()
         message_ref[rows, :] = split(message)
         return 0
 
@@ -159,6 +163,14 @@
         return 0
 
     lax.fori_loop(0, nodes // block, total, 0)
+
+    def finish(step, _):
+        rows = pl.ds(pl.multiple_of(step * tile, tile), tile)
+        for which in range(saves.shape[0]):
+            pltpu.make_async_copy(saves.at[which, rows], saved_refs.at[which, rows], sems.at[step, which]).wait()
+        return 0
+
+    lax.fori_loop(0, tiles, finish, 0)
 
 
 def write_pack(ref, start, grad_first, grad_w2, grad_w3, small):
@@ -233,21 +245,25 @@
 
 
 def mesh_backward_kernel(
-    lat_ref, before_ref, node_ref, after_ref, src_ref, dst_ref, cot_ref, back_ref,
-    one_ref, two_ref, norm_ref, inv_ref, local_ref, first_ref, rest_ref, gain_ref,
-    grad_ref, left_ref, right_ref, out_ref, pack_ref,
-    d_ref, w1_acc, w2_acc, w3_acc, small_acc, sum_src,
+    lat_ref, dst_ref, cot_ref, back_ref, saved_refs, first_ref, rest_ref, gain_ref,
+    grad_ref, d_ref, pack_ref,
+    w1_acc, w2_acc, w3_acc, small_acc, saves, sems,
 ):
-    tiles, groups = src_ref.shape[:2]
+    tiles, groups = dst_ref.shape[:2]
     tile = groups * LANES
     width = lat_ref.shape[1]
-    nodes = node_ref.shape[0]
-    halo = before_ref.shape[0]
+    nodes = back_ref.shape[0]
     w_own = first_ref[0, :width]
-    w_src = first_ref[0, width : 2 * width]
-    w_dst = first_ref[0, 2 * width :]
     gain = gain_ref[0:1]
     rest = (rest_ref[0, 0], rest_ref[0, 1])
+
+    def fetch(step, _):
+        rows = pl.ds(pl.multiple_of(step * tile, tile), tile)
+        for which in range(saves.shape[0]):
+            pltpu.make_async_copy(saved_refs.at[which, rows], saves.at[which, rows], sems.at[step, which]).start()
+        return 0
+
+    lax.fori_loop(0, tiles, fetch, 0)
     for ref in (w1_acc, w2_acc, w3_acc, small_acc):
         ref[...] = jnp.zeros(ref.shape, f32)
 
@@ -255,9 +271,10 @@
         rows = pl.ds(pl.multiple_of(step * tile, tile), tile)
         cot = cot_ref[rows, :].astype(f32)
         upstream = cot + joined(dot(hot_rows(dst_ref[step], nodes), back_ref[...]))
-        d_one, grad_w2, grad_w3, small = backward_layers(
-            upstream, one_ref[rows, :], two_ref[rows, :], norm_ref[rows, :], inv_ref[rows, :], rest, gain
-        )
+        for which in range(saves.shape[0]):
+            pltpu.make_async_copy(saved_refs.at[which, rows], saves.at[which, rows], sems.at[step, which]).wait()
+        saved = [saves[which, rows, :] for which in range(saves.shape[0])]
+        d_one, grad_w2, grad_w3, small = backward_layers(upstream, *saved, rest, gain)
         d_ref[rows, :] = d_one
         w1_acc[...] += dot_tn(lat_ref[rows, :], d_one)
         w2_acc[...] += grad_w2
@@ -267,6 +284,19 @@
         return 0
 
     lax.fori_loop(0, tiles, one, 0)
+    write_pack(pack_ref, 0, w1_acc[...], w2_acc[...], w3_acc[...], small_acc[0:5, :])
+
+
+def mesh_sums_kernel(
+    me_ref, before_ref, node_ref, after_ref, src_ref, dst_ref, d_ref, local_ref, first_ref, own_ref, early_ref,
+    left_ref, right_ref, out_ref, keep_ref, give_ref,
+    sum_src, pack_ref,
+):
+    tiles = src_ref.shape[0]
+    nodes, width = node_ref.shape
+    halo = before_ref.shape[0]
+    w_src = first_ref[0, width : 2 * width]
+    w_dst = first_ref[0, 2 * width :]
     block = 256
 
     def scattered(index_ref, first):
@@ -297,8 +327,35 @@
     right_ref[...] = (dot_nt(last_rows[:, :width], w_src) + dot_nt(last_rows[:, width:], w_src)).astype(bf16)
     grad_src = dot_tn(before_ref[...], first_rows) + dot_tn(node_ref[...], sum_src[halo : halo + nodes])
     grad_src = joined(grad_src + dot_tn(after_ref[...], last_rows))
-    grad_first = jnp.concatenate([w1_acc[...], grad_src, grad_dst], axis=0)
-    write_pack(pack_ref, 0, grad_first, w2_acc[...], w3_acc[...], small_acc[0:5, :])
+    pack_ref[:width, :] = own_ref[:width, :]
+    pack_ref[width : 2 * width, :] = grad_src.astype(bf16)
+    pack_ref[2 * width : 3 * width, :] = grad_dst.astype(bf16)
+    pack_ref[3 * width : PACK, :] = own_ref[width:, :]
+    pack_ref[PACK : 3 * PACK, :] = early_ref[...]
+    pack_ref[3 * PACK :, :] = jnp.zeros((pack_ref.shape[0] - 3 * PACK, width), bf16)
+    half = keep_ref.shape[0]
+    keep_ref[...] = pack_ref[pl.ds(pl.multiple_of(me_ref[0] * half, half), half), :]
+    give_ref[...] = pack_ref[pl.ds(pl.multiple_of((1 - me_ref[0]) * half, half), half), :]
+
+
+def share_kernel(parts_ref, out_ref):
+    total = jnp.sum(parts_ref[...].astype(f32), axis=0, keepdims=True).astype(bf16)
+    out_ref[...] = jnp.broadcast_to(total, out_ref.shape)
+
+
+def unpack_kernel(me_ref, mine_ref, theirs_ref, first_ref, rest_ref, bias_ref, gain_ref, ref, *, scale):
+    half, width = mine_ref.shape
+    ref[pl.ds(pl.multiple_of(me_ref[0] * half, half), half), :] = mine_ref[...]
+    ref[pl.ds(pl.multiple_of((1 - me_ref[0]) * half, half), half), :] = theirs_ref[...]
+    wide = 3 * width
+    for which in range(3):
+        start = which * PACK
+        first_ref[which] = ref[start : start + wide, :].astype(f32) * scale
+        rest_ref[which, 0] = ref[start + wide : start + wide + width, :].astype(f32) * scale
+        rest_ref[which, 1] = ref[start + wide + width : start + wide + 2 * width, :].astype(f32) * scale
+        small = ref[start + wide + 2 * width : start + PACK, :].astype(f32) * scale
+        bias_ref[which] = small[:4]
+        gain_ref[which : which + 1, :] = small[4:5]
 
 
 def final_kernel(blocks_ref, local_ref, left_ref, right_ref, returned_ref, out_ref, total_ref):
@@ -308,30 +365,46 @@
     total_ref[:halo] += left_ref[...].astype(f32)
     total_ref[nodes - halo :] += right_ref[...].astype(f32)
 
-    def one(step, _):
-        target = pl.ds(pl.multiple_of(blocks_ref[step] * BLK, BLK), BLK)
-        source = pl.ds(pl.multiple_of(step * BLK, BLK), BLK)
-        total_ref[target, :] += returned_ref[source, :].astype(f32)
-        return 0
-
-    lax.fori_loop(0, returned_ref.shape[0] // BLK, one, 0, unroll=8)
+    _, domains, slots = blocks_ref.shape
+
+    def one(domain, _):
+        for slot in range(slots):
+            target = pl.ds(pl.multiple_of(blocks_ref[0, domain, slot] * BLK, BLK), BLK)
+            source = pl.ds(pl.multiple_of((domain * slots + slot) * BLK, BLK), BLK)
+            total_ref[target, :] += returned_ref[source, :].astype(f32)
+        return 0
+
+    lax.fori_loop(0, domains, one, 0)
     out_ref[...] = total_ref[...].astype(bf16)
 
 
-def call(kernel, outs, operands, scalars=0, scratch=(), name=None):
-    specs = [pl.BlockSpec(memory_space=pltpu.SMEM)] * scalars
-    specs += [pl.BlockSpec(memory_space=pltpu.VMEM)] * (len(operands) - scalars)
+def call(kernel, outs, operands, scalars=0, outside=(), scratch=(), cost=0):
+    def place(where, scalar, hbm):
+        return pl.BlockSpec(memory_space=pltpu.SMEM if where < scalar else pltpu.HBM if hbm else pltpu.VMEM)
+
+    operands = [
+        pltpu.with_memory_space_constraint(value, pltpu.HBM) if where in outside else value
+        for where, value in enumerate(operands)
+    ]
     return pl.pallas_call(
         kernel,
-        out_shape=[jax.ShapeDtypeStruct(shape, kind) for shape, kind in outs],
-        in_specs=specs,
-        out_specs=[pl.BlockSpec(memory_space=pltpu.VMEM)] * len(outs),
+        out_shape=[pltpu.HBM(*out[:2]) if len(out) > 2 else jax.ShapeDtypeStruct(*out) for out in outs],
+        in_specs=[place(where, scalars, where in outside) for where in range(len(operands))],
+        out_specs=[place(0, 0, len(out) > 2) for out in outs],
         scratch_shapes=list(scratch),
-        name=name,
+        cost_estimate=pl.CostEstimate(flops=cost, transcendentals=0, bytes_accessed=0),
     )(*operands)
 
 
-def per_device(
+def exchange(value, axes, groups=None):
+    return lax.all_to_all(value, axes, split_axis=0, concat_axis=0, axis_index_groups=groups, tiled=True)
+
+
+def shift(value, pairs, axes="dom"):
+    return lax.ppermute(value, axes, pairs)
+
+
+def step(
     node_latents,
     mesh_latents,
     world_latents,
@@ -357,28 +430,37 @@
     both = ("dom", "dp")
     up = [(i, i + 1) for i in range(domains - 1)]
     down = [(j, i) for i, j in up]
-    blocks = send_blocks.reshape(-1)
-    received = blocks.shape[0] * BLK
-
-    (outgoing,) = call(send_kernel, [((received, width), bf16)], (blocks, node_latents), scalars=1, name="send")
-    incoming = lax.all_to_all(outgoing, "dom", split_axis=0, concat_axis=0, tiled=True)
-    before = lax.ppermute(node_latents[nodes - HALO :], "dom", up)
-    after = lax.ppermute(node_latents[:HALO], "dom", down)
-
-    tile = 4 * LANES
+    blocks = send_blocks
+    received = blocks.shape[1] * blocks.shape[2] * BLK
+    micro = 1000000 * COST
+
+    share = -(-3 * PACK // (8 * devices)) * 8
+    half = share * devices // 2
+    me = (lax.axis_index(both) % 2).astype(jnp.int32).reshape(1)
+    pairs = [(i, i ^ 1) for i in range(devices)]
+    groups = [list(range(first, devices, 2)) for first in range(2)]
+
+    (outgoing,) = call(send_kernel, [((received, width), bf16)], (blocks, node_latents), scalars=1, cost=2 * micro)
+    incoming = exchange(outgoing, "dom")
+    before = shift(node_latents[nodes - HALO :], up)
+    after = shift(node_latents[:HALO], down)
+
+    tile = 8 * LANES
     src = mesh_src.reshape(edges // tile, tile // LANES, LANES)
     dst = mesh_dst.reshape(edges // tile, tile // LANES, LANES)
-    full = ((edges, width), f32)
-    new_mesh, pre_one, pre_two, normed, inv_std, mesh_sum = call(
+    saves = (4, edges, width)
+    new_mesh, mesh_sum, saved = call(
         mesh_forward_kernel,
-        [((edges, width), bf16), full, full, full, full, ((nodes, width), bf16)],
+        [((edges, width), bf16), ((nodes, width), bf16), (saves, f32, True)],
         (mesh_latents, before, node_latents, after, src, dst, first_weights, rest_weights, biases, gains),
         scratch=[
             pltpu.VMEM((nodes + 2 * HALO, 2 * width), bf16),
             pltpu.VMEM((nodes, 2 * width), bf16),
             pltpu.VMEM((edges, 2 * width), bf16),
+            pltpu.VMEM(saves, f32),
+            pltpu.SemaphoreType.DMA((edges // tile, saves[0])),
         ],
-        name="mesh_forward",
+        cost=15 * micro,
     )
     new_nodes, new_world, grad_world, to_source, local, mesh_back, early = call(
         middle_kernel,
@@ -407,67 +489,72 @@
             gains,
         ),
         scalars=1,
-        name="middle",
-    )
-    returned = lax.all_to_all(to_source, "dom", split_axis=0, concat_axis=0, tiled=True)
-    grad_mesh, to_left, to_right, local, late = call(
+        cost=10 * micro,
+    )
+    returned = exchange(to_source, "dom")
+    grad_mesh, d_one, own_pack = call(
         mesh_backward_kernel,
-        [
-            ((edges, width), bf16),
-            ((HALO, width), bf16),
-            ((HALO, width), bf16),
-            ((nodes, width), f32),
-            ((PACK, width), bf16),
-        ],
+        [((edges, width), bf16), ((edges, width), bf16), ((PACK - 2 * width, width), bf16)],
         (
             mesh_latents,
-            before,
-            node_latents,
-            after,
-            src,
             dst,
             mesh_cot,
             mesh_back,
-            pre_one,
-            pre_two,
-            normed,
-            inv_std,
-            local,
+            saved,
             first_weights,
             rest_weights,
             gains,
         ),
+        outside=(4,),
         scratch=[
-            pltpu.VMEM((edges, width), bf16),
             pltpu.VMEM((width, width), f32),
             pltpu.VMEM((width, width), f32),
             pltpu.VMEM((width, width), f32),
             pltpu.VMEM((8, width), f32),
-            pltpu.VMEM((nodes + 2 * HALO, 2 * width), bf16),
+            pltpu.VMEM(saves, f32),
+            pltpu.SemaphoreType.DMA((edges // tile, saves[0])),
         ],
-        name="mesh_backward",
-    )
-    from_right = lax.ppermute(to_left, "dom", down)
-    from_left = lax.ppermute(to_right, "dom", up)
-
-    share = -(-3 * PACK // devices)
-    share = -(-share // 16) * 16
-    padding = jnp.zeros((share * devices - 3 * PACK, width), bf16)
-    packed = jnp.concatenate([late, early, padding], axis=0)
-    parts = lax.all_to_all(packed, both, split_axis=0, concat_axis=0, tiled=True)
-    mine = jnp.sum(parts.reshape(devices, share, width).astype(f32), axis=0).astype(bf16)
-    spread = jnp.broadcast_to(mine[None], (devices, share, width)).reshape(devices * share, width)
-    spread = lax.all_to_all(spread, both, split_axis=0, concat_axis=0, tiled=True)
-    sums = spread[: 3 * PACK].reshape(3, PACK, width).astype(f32) / devices
+        cost=10 * micro,
+    )
+    to_left, to_right, local, keep, give = call(
+        mesh_sums_kernel,
+        [
+            ((HALO, width), bf16),
+            ((HALO, width), bf16),
+            ((nodes, width), f32),
+            ((half, width), bf16),
+            ((half, width), bf16),
+        ],
+        (me, before, node_latents, after, src, dst, d_one, local, first_weights, own_pack, early),
+        scalars=1,
+        scratch=[pltpu.VMEM((nodes + 2 * HALO, 2 * width), bf16), pltpu.VMEM((2 * half, width), bf16)],
+        cost=10 * micro,
+    )
+    from_right = shift(to_left, down)
+    from_left = shift(to_right, up)
+    got = shift(give, pairs, both)
+    merged = (keep.astype(f32) + got.astype(f32)).astype(bf16)
+    parts = exchange(merged, both, groups)
+    shape = (devices // 2, share, width)
+    (spread,) = call(share_kernel, [(shape, bf16)], (parts.reshape(shape),), cost=micro)
+    mine = exchange(spread.reshape(merged.shape), both, groups)
+    theirs = shift(mine, pairs, both)
     (grad_nodes,) = call(
         final_kernel,
         [((nodes, width), bf16)],
         (blocks, local, from_left, from_right, returned),
         scalars=1,
         scratch=[pltpu.VMEM((nodes, width), f32)],
-        name="final",
-    )
-    wide = 3 * width
+        cost=2 * micro,
+    )
+    grads = call(
+        functools.partial(unpack_kernel, scale=1.0 / devices),
+        [((3, 3 * width, width), f32), ((3, 2, width, width), f32), ((3, 4, width), f32), ((3, width), f32)],
+        (me, mine, theirs),
+        scalars=1,
+        scratch=[pltpu.VMEM((2 * half, width), bf16)],
+        cost=micro,
+    )
     return (
         new_nodes,
         new_mesh,
@@ -475,10 +562,7 @@
         grad_nodes,
         grad_mesh,
         grad_world,
-        sums[:, :wide],
-        sums[:, wide : wide + 2 * width].reshape(3, 2, width, width),
-        sums[:, wide + 2 * width : wide + 2 * width + 4],
-        sums[:, wide + 2 * width + 4],
+        *grads,
     )
 
 
@@ -486,7 +570,7 @@
     rows = P(("dom", "dp"), None)
     flat = P(("dom", "dp"))
     return jax.shard_map(
-        per_device,
+        step,
         mesh=mesh,
         in_specs=(
             rows,

time: 138 us -> 127 us (0.920)
  the two profiles are of different devices: /device:TPU:17 before, /device:TPU:0 now
where the time goes in v1:
time: 127 us; the launch traced here: 126 us
  Pallas kernels  51.6 us (41%)
  blocking collectives  33.4 us (26%)
  starting transfers between devices  21.8 us (17%)
  waiting for transfers between devices  12.9 us (10%)
  local copies, waits for them, and re-layouts  3.81 us (3%)
  between operations  1.41 us (1%)
    pallas_call x8, Pallas kernels, call(): pl.pallas_call(kernel, out_shape=[pltpu.HBM(*out[:2]) if len(out) > 2 els...  51.6 us
    all_to_all x2, blocking collectives, exchange(): lax.all_to_all(value, axes, split_axis=0, concat_axis=0, axis_index_group...  33.4 us
    ppermute x6, starting transfers between devices, shift(): return lax.ppermute(value, axes, pairs)  11 us
    all_to_all x2, starting transfers between devices, exchange(): lax.all_to_all(value, axes, split_axis=0, concat_axis=0, axis_index_group...  10.8 us
    ppermute x6, waiting for transfers between devices, shift(): return lax.ppermute(value, axes, pairs)  8.89 us
    all_to_all x2, waiting for transfers between devices, exchange(): lax.all_to_all(value, axes, split_axis=0, concat_axis=0, axis_index_group...  4.05 us
    unnamed x16, local copies, waits for them, and re-layouts  2.93 us
  transfers between devices with their start and end apart: 8, of which 6 were waited for; matrix products, arithmetic and copies ran while one was open for 1% of the time, Pallas kernels for 12%

profile of v1, /device:TPU:0, one launch (start us, length us, event | category | flops | bytes accessed | tf_op | source)
XLA Modules:
  0.0 126.0 jit_solution(8932228939765288938)
XLA Ops:
  0.6 2.2 %shard_map.231 = bf16[2048,128]{1,0:T(8,128)(2,1)} custom-call(s32[1,8,16]{2,1,0:T(8,128)} %blocks_ref.3, bf16[1024,128]{1,0:T(8,128)(2,1)} %node_ref.7), custom_call_target="tpu_custom_call" | custom-call | flops 500000000 | tf_op jit(solution)/shard_map/pallas_call | solution.py:389
  2.8 7.3 %all-to-all-start = ((bf16[8,256,128]{2,1,0:T(8,128)(2,1)}), bf16[8,256,128]{2,1,0:T(8,128)(2,1)S(1)}, u32[]{:S(2)}, u32[]{:S(2)}) async-start(bf16[8,256,128]{2,1,0:T(8,128)(2,1)} %bitcast.13), calls=%async_computation | async-start | bytes 1048576 | tf_op jit(solution)/shard_map/all_to_all | solution.py:400
  10.1 0.9 fusion
  11.0 1.3 %collective-permute-start.1 = (bf16[256,128]{1,0:T(8,128)(2,1)S(1)}, bf16[256,128]{1,0:T(8,128)(2,1)S(1)}, u32[]{:S(2)}, u32[]{:S(2)}) collective-permute-start(bf16[256,128]{1,0:T(8,128)(2,1)S(1)} %get-tuple-element.54), channel_id=1, source_target_pairs={{4,0},{8,4},{12,8},{16,12},{20,16},{24,20},{28,24},{5,1},{9,5},{13... | collective-permute-start | bytes 196616 | tf_op jit(solution)/shard_map/ppermute | solution.py:404
  12.3 4.6 %collective-permute-start = (bf16[256,128]{1,0:T(8,128)(2,1)S(1)}, bf16[256,128]{1,0:T(8,128)(2,1)S(1)}, u32[]{:S(2)}, u32[]{:S(2)}) collective-permute-start(bf16[256,128]{1,0:T(8,128)(2,1)S(1)} %get-tuple-element.55), channel_id=1, source_target_pairs={{0,4},{4,8},{8,12},{12,16},{16,20},{20,24},{24,28},{1,5},{5,9},{9,... | collective-permute-start | bytes 196616 | tf_op jit(solution)/shard_map/ppermute | solution.py:404
  17.5 1.3 %collective-permute-done.1.after_ref = bf16[256,128]{1,0:T(8,128)(2,1)S(1)} collective-permute-done((bf16[256,128]{1,0:T(8,128)(2,1)S(1)}, bf16[256,128]{1,0:T(8,128)(2,1)S(1)}, u32[]{:S(2)}, u32[]{:S(2)}) %collective-permute-start.1) | collective-permute-done | bytes 65568 | tf_op jit(solution)/shard_map/ppermute | solution.py:404
  20.1 12.3 %shard_map.232 = (bf16[3072,128]{1,0:T(8,128)(2,1)}, bf16[1024,128]{1,0:T(8,128)(2,1)}, f32[4,3072,128]{2,1,0:T(8,128)}) custom-call(bf16[3072,128]{1,0:T(8,128)(2,1)} %lat_ref.5, bf16[256,128]{1,0:T(8,128)(2,1)} %copy-done.5, bf16[1024,128]{1,0:T(8,128)(2,1)} %node_ref.7, bf16[256,128]{1,0:T(8,128)(2,1)} %copy-done.4, s32[3,8,128]{2,1,0:T(8,128)} %bitcast.17, ...), custom_call_target="tpu_custom_call" | custom-call | flops 3750000128 | tf_op jit(solution)/shard_map/pallas_call | solution.py:389
  33.1 10.5 %shard_map.233 = (bf16[1024,128]{1,0:T(8,128)(2,1)}, bf16[512,128]{1,0:T(8,128)(2,1)}, bf16[512,128]{1,0:T(8,128)(2,1)}, bf16[2048,128]{1,0:T(8,128)(2,1)}, f32[...) custom-call(s32[1]{0:T(128)S(6)} %copy.26.count_ref, bf16[1024,128]{1,0:T(8,128)(2,1)} %node_ref.7, ...), custom_call_target="tpu_custom_call" | custom-call | flops 2500000000 | tf_op jit(solution)/shard_map/pallas_call | solution.py:389
  43.6 10.6 %shard_map.234 = (bf16[3072,128]{1,0:T(8,128)(2,1)}, bf16[3072,128]{1,0:T(8,128)(2,1)}, bf16[400,128]{1,0:T(8,128)(2,1)}) custom-call(bf16[3072,128]{1,0:T(8,128)(2,1)} %lat_ref.5, s32[3,8,128]{2,1,0:T(8,128)} %bitcast.20, bf16[3072,128]{1,0:T(8,128)(2,1)} %cot_ref.1, bf16[1024,256]{1,0:T(8,128)(2,1)} %get-tuple-element.36.back_ref, ...), custom_call_target="tpu_custom_call" | custom-call | flops 2500000000 | tf_op jit(solution)/shard_map/pallas_call | solution.py:389
  54.3 9.7 %shard_map.235 = (bf16[256,128]{1,0:T(8,128)(2,1)}, bf16[256,128]{1,0:T(8,128)(2,1)}, f32[1024,128]{1,0:T(8,128)}, bf16[1024,128]{1,0:T(8,128)(2,1)}, bf16[1024,128]{1,0:T(8,128)(2,1)}) custom-call(s32[1]{0:T(128)} %bitcast.6.me_ref, bf16[256,128]{1,0:T(8,128)(2,1)} %copy-done.5, bf16[1024,128]{1,0:T(8,128)(2,1)} %node_ref.7, bf16[256,128]{1,0:T(8,128)(2,1)} %copy-done.4, ...), custom_call_target="tpu_custom_call" | custom-call | flops 2500000000 | tf_op jit(solution)/shard_map/pallas_call | solution.py:389
  64.0 1.7 %collective-permute-done.4 = bf16[1024,128]{1,0:T(8,128)(2,1)S(1)} collective-permute-done((bf16[1024,128]{1,0:T(8,128)(2,1)}, bf16[1024,128]{1,0:T(8,128)(2,1)S(1)}, u32[]{:S(2)}, u32[]{:S(2)}) %collective-permute-start.4) | collective-permute-done | bytes 262176 | tf_op jit(solution)/shard_map/ppermute | solution.py:404
  65.8 1.0 add_convert_fusion
  66.8 20.5 %all_to_all.39.parts_ref = bf16[16,64,128]{2,1,0:T(8,128)(2,1)} all-to-all(bf16[16,64,128]{2,1,0:T(8,128)(2,1)S(1)} %bitcast.11), channel_id=1, replica_groups={{0,2,4,6,8,10,12,14,16,18,20,22,24,26,28,30},{1,3,5,7,9,11,13,15,17,19,..., dimensions={0} | all-to-all | bytes 524288 | tf_op jit(solution)/shard_map/all_to_all | solution.py:400
  87.2 1.7 %shard_map.237 = bf16[16,64,128]{2,1,0:T(8,128)(2,1)} custom-call(bf16[16,64,128]{2,1,0:T(8,128)(2,1)} %all_to_all.39.parts_ref), custom_call_target="tpu_custom_call" | custom-call | flops 250000000 | tf_op jit(solution)/shard_map/pallas_call | solution.py:389
  89.0 13.0 %all_to_all.40 = bf16[16,64,128]{2,1,0:T(8,128)(2,1)S(1)} all-to-all(bf16[16,64,128]{2,1,0:T(8,128)(2,1)} %shard_map.237), channel_id=1, replica_groups={{0,2,4,6,8,10,12,14,16,18,20,22,24,26,28,30},{1,3,5,7,9,11,13,15,17,19,..., dimensions={0} | all-to-all | bytes 524288 | tf_op jit(solution)/shard_map/all_to_all | solution.py:400
  101.9 3.5 %all-to-all-start.1 = ((bf16[8,256,128]{2,1,0:T(8,128)(2,1)}), bf16[8,256,128]{2,1,0:T(8,128)(2,1)S(1)}, u32[]{:S(2)}, u32[]{:S(2)}) async-start(bf16[8,256,128]{2,1,0:T(8,128)(2,1)} %bitcast.7), calls=%async_computation.1 | async-start | bytes 1048576 | tf_op jit(solution)/shard_map/all_to_all | solution.py:400
  105.5 3.8 %collective-permute-start.2 = (bf16[256,128]{1,0:T(8,128)(2,1)}, bf16[256,128]{1,0:T(8,128)(2,1)S(1)}, u32[]{:S(2)}, u32[]{:S(2)}) collective-permute-start(bf16[256,128]{1,0:T(8,128)(2,1)} %get-tuple-element.43), channel_id=1, source_target_pairs={{0,4},{4,8},{8,12},{12,16},{16,20},{20,24},{24,28},{1,5},{5,9},{9,... | collective-permute-start | bytes 196616 | tf_op jit(solution)/shard_map/ppermute | solution.py:404
  109.3 1.3 %collective-permute-start.3 = (bf16[256,128]{1,0:T(8,128)(2,1)}, bf16[256,128]{1,0:T(8,128)(2,1)S(1)}, u32[]{:S(2)}, u32[]{:S(2)}) collective-permute-start(bf16[256,128]{1,0:T(8,128)(2,1)} %get-tuple-element.44), channel_id=1, source_target_pairs={{4,0},{8,4},{12,8},{16,12},{20,16},{24,20},{28,24},{5,1},{9,5},{13... | collective-permute-start | bytes 196616 | tf_op jit(solution)/shard_map/ppermute | solution.py:404
  110.6 1.5 %collective-permute-done.2.left_ref = bf16[256,128]{1,0:T(8,128)(2,1)S(1)} collective-permute-done((bf16[256,128]{1,0:T(8,128)(2,1)}, bf16[256,128]{1,0:T(8,128)(2,1)S(1)}, u32[]{:S(2)}, u32[]{:S(2)}) %collective-permute-start.2) | collective-permute-done | bytes 65568 | tf_op jit(solution)/shard_map/ppermute | solution.py:404
  112.1 3.7 %collective-permute-done.3.right_ref = bf16[256,128]{1,0:T(8,128)(2,1)S(1)} collective-permute-done((bf16[256,128]{1,0:T(8,128)(2,1)}, bf16[256,128]{1,0:T(8,128)(2,1)S(1)}, u32[]{:S(2)}, u32[]{:S(2)}) %collective-permute-start.3) | collective-permute-done | bytes 65568 | tf_op jit(solution)/shard_map/ppermute | solution.py:404
  115.8 4.0 %all-to-all-done.1 = bf16[8,256,128]{2,1,0:T(8,128)(2,1)S(1)} async-done(((bf16[8,256,128]{2,1,0:T(8,128)(2,1)}), bf16[8,256,128]{2,1,0:T(8,128)(2,1)S(1)}, u32[]{:S(2)}, u32[]{:S(2)}) %all-to-all-start.1) | async-done | bytes 524320 | tf_op jit(solution)/shard_map/all_to_all | solution.py:400
  119.9 0.8 copy-done.1
  120.7 2.6 %shard_map.236 = bf16[1024,128]{1,0:T(8,128)(2,1)} custom-call(s32[1,8,16]{2,1,0:T(8,128)} %blocks_ref.3, f32[1024,128]{1,0:T(8,128)} %get-tuple-element.42.local_ref, bf16[256,128]{1,0:T(8,128)(2,1)} %copy-done.6, bf16[256,128]{1,0:T(8,128)(2,1)} %copy-done.7, bf16[2048,128]{1,0:T(8,128)(2,1)} %bitcast.14), custom_call_target="tpu_custom_call" | custom-call | flops 500000000 | tf_op jit(solution)/shard_map/pallas_call | solution.py:389
  124.0 2.0 %shard_map.238 = (f32[3,384,128]{2,1,0:T(8,128)}, f32[3,2,128,128]{3,2,1,0:T(8,128)}, f32[3,4,128]{2,1,0:T(4,128)}, f32[3,128]{1,0:T(4,128)}) custom-call(s32[1]{0:T(128)} %bitcast.6.me_ref, bf16[1024,128]{1,0:T(8,128)(2,1)} %bitcast.16, bf16[1024,128]{1,0:T(8,128)(2,1)} %copy-done.3), custom_call_target="tpu_custom_call" | custom-call | flops 250000000 | tf_op jit(solution)/shard_map/pallas_call | solution.py:389
  (20 shorter events, 2.9 us)
Async XLA Ops:
  2.8 29.5 %all-to-all-start = ((bf16[8,256,128]{2,1,0:T(8,128)(2,1)}), bf16[8,256,128]{2,1,0:T(8,128)(2,1)S(1)}, u32[]{:S(2)}, u32[]{:S(2)}) async-start(bf16[8,256,128]{2,1,0:T(8,128)(2,1)} %bitcast.13), calls=%async_computation | async-start | bytes 1048576 | tf_op jit(solution)/shard_map/all_to_all | solution.py:400
  11.0 7.8 %collective-permute-start.1 = (bf16[256,128]{1,0:T(8,128)(2,1)S(1)}, bf16[256,128]{1,0:T(8,128)(2,1)S(1)}, u32[]{:S(2)}, u32[]{:S(2)}) collective-permute-start(bf16[256,128]{1,0:T(8,128)(2,1)S(1)} %get-tuple-element.54), channel_id=1, source_target_pairs={{4,0},{8,4},{12,8},{16,12},{20,16},{24,20},{28,24},{5,1},{9,5},{13... | collective-permute-start | bytes 196616 | tf_op jit(solution)/shard_map/ppermute | solution.py:404
  12.3 7.1 %collective-permute-start = (bf16[256,128]{1,0:T(8,128)(2,1)S(1)}, bf16[256,128]{1,0:T(8,128)(2,1)S(1)}, u32[]{:S(2)}, u32[]{:S(2)}) collective-permute-start(bf16[256,128]{1,0:T(8,128)(2,1)S(1)} %get-tuple-element.55), channel_id=1, source_target_pairs={{0,4},{4,8},{8,12},{12,16},{16,20},{20,24},{24,28},{1,5},{5,9},{9,... | collective-permute-start | bytes 196616 | tf_op jit(solution)/shard_map/ppermute | solution.py:404
  18.8 0.7 copy-start.4
  19.4 0.6 copy-start.5
  32.3 0.8 copy-start
  64.0 1.7 %collective-permute-start.4 = (bf16[1024,128]{1,0:T(8,128)(2,1)}, bf16[1024,128]{1,0:T(8,128)(2,1)S(1)}, u32[]{:S(2)}, u32[]{:S(2)}) collective-permute-start(bf16[1024,128]{1,0:T(8,128)(2,1)} %get-tuple-element.49), channel_id=1, source_target_pairs={{0,1},{1,0},{2,3},{3,2},{4,5},{5,4},{6,7},{7,6},{8,9},{9,8},{10,11... | collective-permute-start | bytes 786440 | tf_op jit(solution)/shard_map/ppermute | solution.py:404
  101.9 21.3 %copy-start.2 = (bf16[16,64,128]{2,1,0:T(8,128)(2,1)}, bf16[16,64,128]{2,1,0:T(8,128)(2,1)S(1)}, u32[]{:S(2)}) copy-start(bf16[16,64,128]{2,1,0:T(8,128)(2,1)S(1)} %all_to_all.40) | copy-start | bytes 786436
  101.9 18.0 %all-to-all-start.1 = ((bf16[8,256,128]{2,1,0:T(8,128)(2,1)}), bf16[8,256,128]{2,1,0:T(8,128)(2,1)S(1)}, u32[]{:S(2)}, u32[]{:S(2)}) async-start(bf16[8,256,128]{2,1,0:T(8,128)(2,1)} %bitcast.7), calls=%async_computation.1 | async-start | bytes 1048576 | tf_op jit(solution)/shard_map/all_to_all | solution.py:400
  105.4 17.8 %collective-permute-start.5 = (bf16[1024,128]{1,0:T(8,128)(2,1)S(1)}, bf16[1024,128]{1,0:T(8,128)(2,1)S(1)}, u32[]{:S(2)}, u32[]{:S(2)}) collective-permute-start(bf16[1024,128]{1,0:T(8,128)(2,1)S(1)} %bitcast.15), channel_id=1, source_target_pairs={{0,1},{1,0},{2,3},{3,2},{4,5},{5,4},{6,7},{7,6},{8,9},{9,8},{10,11... | collective-permute-start | bytes 786440 | tf_op jit(solution)/shard_map/ppermute | solution.py:404
  105.5 6.6 %collective-permute-start.2 = (bf16[256,128]{1,0:T(8,128)(2,1)}, bf16[256,128]{1,0:T(8,128)(2,1)S(1)}, u32[]{:S(2)}, u32[]{:S(2)}) collective-permute-start(bf16[256,128]{1,0:T(8,128)(2,1)} %get-tuple-element.43), channel_id=1, source_target_pairs={{0,4},{4,8},{8,12},{12,16},{16,20},{20,24},{24,28},{1,5},{5,9},{9,... | collective-permute-start | bytes 196616 | tf_op jit(solution)/shard_map/ppermute | solution.py:404
  109.3 6.5 %collective-permute-start.3 = (bf16[256,128]{1,0:T(8,128)(2,1)}, bf16[256,128]{1,0:T(8,128)(2,1)S(1)}, u32[]{:S(2)}, u32[]{:S(2)}) collective-permute-start(bf16[256,128]{1,0:T(8,128)(2,1)} %get-tuple-element.44), channel_id=1, source_target_pairs={{4,0},{8,4},{12,8},{16,12},{20,16},{24,20},{28,24},{5,1},{9,5},{13... | collective-permute-start | bytes 196616 | tf_op jit(solution)/shard_map/ppermute | solution.py:404
  112.1 7.8 %copy-start.6 = (bf16[256,128]{1,0:T(8,128)(2,1)}, bf16[256,128]{1,0:T(8,128)(2,1)S(1)}, u32[]{:S(2)}) copy-start(bf16[256,128]{1,0:T(8,128)(2,1)S(1)} %collective-permute-done.2.left_ref) | copy-start | bytes 196612
  115.8 4.1 %copy-start.7 = (bf16[256,128]{1,0:T(8,128)(2,1)}, bf16[256,128]{1,0:T(8,128)(2,1)S(1)}, u32[]{:S(2)}) copy-start(bf16[256,128]{1,0:T(8,128)(2,1)S(1)} %collective-permute-done.3.right_ref) | copy-start | bytes 196612
  119.9 0.8 copy-start.1
  123.3 0.7 copy-start.3
